TPU v7x, 32 devices: a whole 2x2x4 slice. The times are simulated.
32 devices in a mesh: dp: 8 (over z, y), tp: 4 (over x, core).
Axes of the slice: x: 2, y: 2, z: 4, core: 2. Of those that a mesh axis runs over, the one named last changes fastest.
Arguments:
- partial_up: bfloat16 [8, 1024, 4096], P('dp', None, 'tp'), may hold values from -4 to 4
- partial_down: bfloat16 [8, 4096, 1024], P('dp', 'tp'), may hold values from -4 to 4
- partial_norm: bfloat16 [8, 1024], P('dp'), may hold values from -8 to 8
- master_up: float32 [1024, 4096], P('dp', 'tp'), may hold values from -0.25 to 0.25
- master_down: float32 [4096, 1024], P('tp', 'dp'), may hold values from -0.125 to 0.125
- master_norm: float32 [1024], P('dp'), may hold values from 0.25 to 1.75
- memory_up: float32 [1024, 4096], P('dp', 'tp'), may hold values from 0.0001953125 to 0.001953125
- memory_down: float32 [4096, 1024], P('tp', 'dp'), may hold values from 4.8828126e-05 to 0.00048828125
- memory_norm: float32 [1024], P('dp'), may hold values from 0.05 to 0.8
Outputs:
- compute_up: bfloat16 [1024, 4096], P(None, 'tp')
- compute_down: bfloat16 [4096, 1024], P('tp')
- compute_norm: bfloat16 [1024], replicated
- stepped_up: float32 [1024, 4096], P('dp', 'tp')
- stepped_down: float32 [4096, 1024], P('tp', 'dp')
- stepped_norm: float32 [1024], P('dp')
- state_new_up: float32 [1024, 4096], P('dp', 'tp')
- state_new_down: float32 [4096, 1024], P('tp', 'dp')
- state_new_norm: float32 [1024], P('dp')
All inputs are finite; a program needn't handle non-finite values.
Results may differ from a plain program's by a relative error of at most 0.001.
Values may be sent and summed in bfloat16 or wider, within the bound.
A program may use at most 64 MiB of HBM per device.

v0:
```python
import jax
import jax.numpy as jnp
from jax import lax
from jax.sharding import PartitionSpec as P

learn_rate = 0.025
hold_rate = 0.8


def local(
    partial_up,
    partial_down,
    partial_norm,
    master_up,
    master_down,
    master_norm,
    memory_up,
    memory_down,
    memory_norm,
):
    mean_up, mean_down, mean_norm = (
        lax.psum_scatter(partial_up[0].astype(jnp.float32), "dp", scatter_dimension=0, tiled=True),
        lax.psum_scatter(
            partial_down[0].astype(jnp.float32), "dp", scatter_dimension=1, tiled=True
        ),
        lax.psum_scatter(
            partial_norm[0].astype(jnp.float32), "dp", scatter_dimension=0, tiled=True
        ),
    )
    mean_rate = lax.axis_size("dp") ** (-0.5)
    mean_up = mean_up * mean_rate
    mean_down = mean_down * mean_rate
    mean_norm = mean_norm * mean_rate
    own_up, own_down, slope_up_norm, slope_down_norm = lax.psum(
        (
            jnp.sum(master_up * master_up, axis=1, keepdims=True),
            jnp.sum(master_down * master_down, axis=0, keepdims=True),
            jnp.sum(mean_up * mean_up, axis=1, keepdims=True),
            jnp.sum(mean_down * mean_down, axis=0, keepdims=True),
        ),
        "tp",
    )
    mean_up = mean_up * (jnp.sqrt(own_up) * lax.rsqrt(slope_up_norm + 1e-06))
    mean_down = mean_down * (jnp.sqrt(own_down) * lax.rsqrt(slope_down_norm + 1e-06))
    state_new_up = hold_rate * memory_up + (1.0 - hold_rate) * mean_up * mean_up
    stepped_up = master_up - learn_rate * mean_up * lax.rsqrt(state_new_up + 1e-06)
    state_new_down = hold_rate * memory_down + (1.0 - hold_rate) * mean_down * mean_down
    stepped_down = master_down - learn_rate * mean_down * lax.rsqrt(state_new_down + 1e-06)
    state_new_norm = hold_rate * memory_norm + (1.0 - hold_rate) * mean_norm * mean_norm
    stepped_norm = master_norm - learn_rate * mean_norm * lax.rsqrt(state_new_norm + 1e-06)
    compute_up, compute_down, compute_norm = (
        lax.all_gather(stepped_up.astype(jnp.bfloat16), "dp", axis=0, tiled=True),
        lax.all_gather(stepped_down.astype(jnp.bfloat16), "dp", axis=1, tiled=True),
        lax.all_gather(stepped_norm.astype(jnp.bfloat16), "dp", axis=0, tiled=True),
    )
    return (
        compute_up,
        compute_down,
        compute_norm,
        stepped_up,
        stepped_down,
        stepped_norm,
        state_new_up,
        state_new_down,
        state_new_norm,
    )


def solution(mesh):
    return jax.shard_map(
        local,
        mesh=mesh,
        in_specs=(
            P("dp", None, "tp"),
            P("dp", "tp", None),
            P("dp", None),
            P("dp", "tp"),
            P("tp", "dp"),
            P("dp"),
            P("dp", "tp"),
            P("tp", "dp"),
            P("dp"),
        ),
        out_specs=(
            P(None, "tp"),
            P("tp", None),
            P(),
            P("dp", "tp"),
            P("tp", "dp"),
            P("dp"),
            P("dp", "tp"),
            P("tp", "dp"),
            P("dp"),
        ),
        check_vma=False,
    )
```

profile of v0, /device:TPU:0, one launch (start us, length us, event | category | flops | bytes accessed | tf_op | source)
XLA Modules:
  0.0 315.5 jit_solution(7703782272232173256)
XLA Ops:
  7.2 0.0 reduce-scatter.3.cloned.1.call-start
  7.2 4.0 %bitcast_convert_fusion.1 = f32[1024,1024]{1,0:T(8,128)} fusion(bf16[1,1024,1024]{2,1,0:T(8,128)(2,1)} %param.9), kind=kLoop, calls=%fused_computation.1 | loop fusion | flops 1048576 | bytes 6291456 | tf_op jit(solution)/shard_map/convert_element_type | solution.py:22
  11.2 0.0 copy-start
  11.2 0.0 reduce-scatter.3.cloned.1.call-update
  11.2 0.0 reduce-scatter.5.cloned.1.call-start
  11.3 1.5 copy-done
  12.8 2.4 bitcast_convert_fusion
  15.2 0.0 copy-start.3
  15.2 0.0 copy-start.2
  15.2 0.0 reduce-scatter.5.cloned.1.call-update
  15.3 0.0 copy-start.5
  15.3 0.0 all-gather.6.cloned.1.call-start
  15.3 1.0 copy-done.3
  16.3 0.1 multiply_reduce_fusion.3
  16.4 0.0 copy-done.2
  16.4 0.1 multiply_reduce_fusion.1
  16.6 0.0 copy-start.6
  16.6 86.1 %reduce-scatter.3.cloned.1.call-done = f32[128,1024]{1,0:T(8,128)} async-done(((f32[1024,1024]{1,0:T(8,128)}), f32[128,1024]{1,0:T(8,128)}) %reduce-scatter.3.cloned.1.call-update) | async-done | bytes 524304 | tf_op jit(solution)/shard_map/reduce_scatter | solution.py:22
  102.7 0.0 copy-start.4
  102.7 1.2 multiply_reduce_fusion.2
  103.9 90.7 %reduce-scatter.5.cloned.1.call-done = f32[1024,128]{1,0:T(8,128)} async-done(((f32[1024,1024]{1,0:T(8,128)}), f32[1024,128]{1,0:T(8,128)}) %reduce-scatter.5.cloned.1.call-update) | async-done | bytes 524304 | tf_op jit(solution)/shard_map/reduce_scatter | solution.py:23
  194.6 1.2 multiply_reduce_fusion
  195.8 6.2 %all-reduce.1 = (f32[128,1]{0,1:T(1,128)S(1)}, f32[128,1]{0,1:T(1,128)S(1)}, f32[1,128]{1,0:T(1,128)S(1)}, f32[1,128]{1,0:T(1,128)S(1)}) all-reduce(f32[128,1]{0,1:T(1,128)S(1)} %bitcast.22, f32[128,1]{0,1:T(1,128)S(1)} %bitcast.20, f32[1,128]{1,0:T(1,128)S(1)} %bitcast.23, ...), channel_id=1, replica_groups=mesh['dp'=8,'tp'=4] {'tp'}, use_global_device_ids=true, to_apply=%region_4.0 | all-reduce | flops 512 | bytes 4096 | tf_op jit(solution)/shard_map/psum | solution.py:34
  202.1 0.0 copy-done.5
  202.1 2.3 fusion.2
  204.3 0.0 copy-start.7
  204.3 0.0 copy-start.10
  204.3 0.0 copy-start.8
  204.3 0.0 all-gather.6.cloned.1.call-update
  204.4 0.0 all-gather.4.cloned.1.call-start
  204.4 0.0 copy-done.6
  204.4 0.0 copy-done.4
  204.4 1.3 fusion.4
  205.7 0.0 all-gather.4.cloned.1.call-update
  205.8 0.0 copy-done.7
  205.8 0.0 copy-done.10
  205.8 0.6 dynamic-slice
  207.0 21.0 %all-reduce = f32[1024]{0:T(1024)S(1)} all-reduce(f32[1024]{0:T(1024)S(1)} %bitcast.19), channel_id=4, replica_groups=mesh['dp'=8,'tp'=4] {'dp'}, use_global_device_ids=true, to_apply=%region_10.0.clone | all-reduce | flops 1024 | bytes 8192
  228.1 0.0 copy-done.8
  228.1 0.0 copy-done.9
  228.1 0.6 convert_bitcast_fusion
  228.7 16.5 %all-gather = bf16[8,1,128]{2,1,0:T(2,128)(2,1)S(1)} all-gather(bf16[1,1,128]{2,1,0:T(2,128)(2,1)S(1)} %get-tuple-element.13), channel_id=1, replica_groups=mesh['dp'=8,'tp'=4] {'dp'}, dimensions={0}, use_global_device_ids=true | all-gather | bytes 2304 | tf_op jit(solution)/shard_map/all_gather | solution.py:54
  245.2 0.6 reduce
  245.8 8.7 %all-gather.6.cloned.1.call-done = bf16[1024,1024]{1,0:T(8,128)(2,1)} async-done(((bf16[1024,128]{1,0:T(8,128)(2,1)}), bf16[1024,1024]{1,0:T(8,128)(2,1)}) %all-gather.6.cloned.1.call-update) | async-done | bytes 2097168 | tf_op jit(solution)/shard_map/all_gather | solution.py:53
  254.6 49.9 %all-gather.4.cloned.1.call-done = bf16[1024,1024]{1,0:T(8,128)(2,1)} async-done(((bf16[128,1024]{1,0:T(8,128)(2,1)}), bf16[1024,1024]{1,0:T(8,128)(2,1)}) %all-gather.4.cloned.1.call-update) | async-done | bytes 2097168 | tf_op jit(solution)/shard_map/all_gather | solution.py:52
  304.4 3.2 %copy.20 = bf16[1024,1024]{1,0:T(8,128)(2,1)} copy(bf16[1024,1024]{1,0:T(8,128)(2,1)} %all-gather.4.cloned.1.call-done) | data formatting | bytes 4194304
  307.6 0.0 copy-done.1
  307.6 1.3 copy.21
  (5 shorter events, 0.0 us)
Async XLA Ops:
  7.2 95.5 %reduce-scatter.3.cloned.1.call-start = ((), (), s32[]{:S(2)}) async-start(), calls=%async_computation.2 | async-start | bytes 4718592 | tf_op jit(solution)/shard_map/reduce_scatter | solution.py:22
  11.2 1.6 copy-start
  11.2 183.4 %reduce-scatter.5.cloned.1.call-start = ((), (), s32[]{:S(2)}) async-start(), calls=%async_computation.4 | async-start | bytes 4718592 | tf_op jit(solution)/shard_map/reduce_scatter | solution.py:23
  15.2 1.0 copy-start.3
  15.2 1.2 copy-start.2
  15.3 186.8 %copy-start.5 = (f32[1024,128]{1,0:T(8,128)S(1)}, f32[1024,128]{1,0:T(8,128)}, u32[]{:S(2)}) copy-start(f32[1024,128]{1,0:T(8,128)} %param.16) | copy-start | bytes 1572868
  15.3 239.3 %all-gather.6.cloned.1.call-start = ((), (), s32[]{:S(2)}) async-start(), calls=%async_computation.5 | async-start | bytes 2359296 | tf_op jit(solution)/shard_map/all_gather | solution.py:53
  16.6 187.8 %copy-start.6 = (f32[128,1024]{1,0:T(8,128)S(1)}, f32[128,1024]{1,0:T(8,128)}, u32[]{:S(2)}) copy-start(f32[128,1024]{1,0:T(8,128)} %param.15) | copy-start | bytes 1572868
  102.7 101.7 %copy-start.4 = (f32[128,1024]{1,0:T(8,128)S(1)}, f32[128,1024]{1,0:T(8,128)}, u32[]{:S(2)}) copy-start(f32[128,1024]{1,0:T(8,128)} %reduce-scatter.3.cloned.1.call-done) | copy-start | bytes 1572868
  204.3 1.4 copy-start.7
  204.3 1.5 copy-start.10
  204.3 23.8 %copy-start.8 = (f32[128]{0:T(128)S(1)}, f32[128]{0:T(128)}, u32[]{:S(2)}) copy-start(f32[128]{0:T(128)} %param.14) | copy-start | bytes 1540
  204.3 23.8 %copy-start.9 = (f32[128]{0:T(128)S(1)}, f32[128]{0:T(128)}, u32[]{:S(2)}) copy-start(f32[128]{0:T(128)} %param.17) | copy-start | bytes 1540
  204.4 100.1 %all-gather.4.cloned.1.call-start = ((), (), s32[]{:S(2)}) async-start(), calls=%async_computation.3 | async-start | bytes 2359296 | tf_op jit(solution)/shard_map/all_gather | solution.py:52
  304.4 3.2 %copy-start.1 = (bf16[1024,1024]{1,0:T(8,128)(2,1)S(1)}, bf16[1024,1024]{1,0:T(8,128)(2,1)}, u32[]{:S(2)}) copy-start(bf16[1024,1024]{1,0:T(8,128)(2,1)} %all-gather.6.cloned.1.call-done) | copy-start | bytes 6291460
Sparse Core Ops, SparseCore 0:
  11.6 91.0 reduce-scatter.2
  106.3 88.2 reduce-scatter.4
  204.5 50.0 all-gather.5
  257.1 47.2 all-gather.3
where the time goes:
time: 316 us; the launch traced here: 315 us
  waiting for transfers between devices  235 us (74%)
  blocking collectives  43.8 us (14%)
  between operations  14.5 us (5%)
  other arithmetic  13.9 us (4%)
  local copies, waits for them, and re-layouts  7.68 us (2%)
    reduce_scatter x1, waiting for transfers between devices, local(): lax.psum_scatter(partial_down[0].astype(jnp.float32), 'dp', scatter_dimen...  90.7 us
    reduce_scatter x1, waiting for transfers between devices, local(): lax.psum_scatter(partial_up[0].astype(jnp.float32), 'dp', scatter_dimensi...  86.1 us
    all_gather x1, waiting for transfers between devices, local(): lax.all_gather(stepped_up.astype(jnp.bfloat16), 'dp', axis=0, tiled=True)  49.9 us
    unnamed x1, blocking collectives  21 us
    all_gather x1, blocking collectives, local(): lax.all_gather(stepped_norm.astype(jnp.bfloat16), 'dp', axis=0, tiled=True)  16.5 us
    all_gather x1, waiting for transfers between devices, local(): lax.all_gather(stepped_down.astype(jnp.bfloat16), 'dp', axis=1, tiled=True)  8.74 us
    unnamed x25, local copies, waits for them, and re-layouts  7.68 us
  transfers between devices with their start and end apart: 4, of which 4 were waited for; matrix products, arithmetic and copies ran while one was open for 2% of the time, Pallas kernels for 0%

commit v1 on v0

--- a/solution.py
+++ b/solution.py
@@ -1,10 +1,299 @@
+import functools
+
 import jax
 import jax.numpy as jnp
 from jax import lax
+from jax.experimental import pallas as pl
+from jax.experimental.pallas import tpu as pltpu
 from jax.sharding import PartitionSpec as P
 
 learn_rate = 0.025
 hold_rate = 0.8
+f32 = jnp.float32
+bf16 = jnp.bfloat16
+MESH = pl.DeviceIdType.MESH
+
+
+def kernel(
+    n, T, Y, K,
+    pd, pu, pn, md, ed, mu, eu,
+    cd, cu, cn, sd, su, sn, td, tu, tn,
+    rd, ru, rn, totd, totu, nsend, nrecv,
+    loc, nms, nmr, rss, rsr, nxs, nxr, azs, azr, ays, ayr,
+):
+    Z = n // Y
+    me = lax.axis_index("dp")
+    tp = lax.axis_index("tp")
+    z, y = me // Y, me % Y
+    W = rd.shape[2]
+    R = ru.shape[1]
+    H = rd.shape[1]
+    rc = R // K
+    rate = n ** -0.5
+
+    def remote(src, dst, s, r, dev):
+        return pltpu.make_async_remote_copy(
+            src_ref=src, dst_ref=dst, send_sem=s, recv_sem=r, device_id=dev, device_id_type=MESH
+        )
+
+    def up(a, m):
+        return pl.multiple_of(a, m)
+
+    peers = [lax.rem(me + o, n) for o in range(1, n)]
+    tpeers = [lax.rem(tp + o, T) for o in range(1, T)]
+
+    def src_of(c, d):
+        if c == 0:
+            return pd.at[0, :, pl.ds(up(d * W, 128), W)]
+        return pu.at[0, pl.ds(up(d * R + (c - 1) * rc, 16), rc), :]
+
+    def slot_of(c, s):
+        if c == 0:
+            return rd.at[s]
+        return ru.at[s, pl.ds((c - 1) * rc, rc), :]
+
+    def block_of(c, d):
+        if c == 0:
+            return cd.at[:, pl.ds(up(d * W, 128), W)]
+        return cu.at[pl.ds(up(d * R + (c - 1) * rc, 16), rc), :]
+
+    def local_copy(c):
+        return pltpu.make_async_copy(src_of(c, me), slot_of(c, me), loc.at[c])
+
+    def rs_copy(c, o, d):
+        return remote(src_of(c, d), slot_of(c, me), rss.at[c, o], rsr.at[c, me], (d, tp))
+
+    def rs_start(c):
+        for o, d in enumerate(peers):
+            rs_copy(c, o, d).start()
+
+    def rs_wait(c):
+        local_copy(c).wait()
+        for s in peers:
+            remote(slot_of(c, s), slot_of(c, s), rss.at[c, 0], rsr.at[c, s], (s, tp)).wait_recv()
+
+    def nx_copy(c, o, t):
+        return remote(nsend.at[c], nrecv.at[c, tp], nxs.at[c, o], nxr.at[c, tp], (me, t))
+
+    def exchange(c, value):
+        nsend[c] = value
+        nrecv[c, tp] = value
+        for o, t in enumerate(tpeers):
+            nx_copy(c, o, t).start()
+        for t in tpeers:
+            remote(nsend.at[c], nrecv.at[c, t], nxs.at[c, 0], nxr.at[c, t], (me, t)).wait_recv()
+        total = nrecv[c, 0]
+        for t in range(1, T):
+            total = total + nrecv[c, t]
+        return total
+
+    def update(m, master, memory):
+        state = hold_rate * memory + (1.0 - hold_rate) * m * m
+        return state, master - learn_rate * m * lax.rsqrt(state + 1e-06)
+
+    def down():
+        c, hb = 0, 128
+        def add(i, carry):
+            rows = pl.ds(up(i * hb, hb), hb)
+            acc = rd[0, rows, :].astype(f32)
+            for s in range(1, n):
+                acc = acc + rd[s, rows, :].astype(f32)
+            acc = acc * rate
+            totd[rows, :] = acc
+            w = md[rows, :]
+            return (
+                carry[0] + jnp.sum((w * w).reshape(hb // 8, 8, W), axis=0),
+                carry[1] + jnp.sum((acc * acc).reshape(hb // 8, 8, W), axis=0),
+            )
+        zero = jnp.zeros((8, W), f32)
+        own, slope = lax.fori_loop(0, H // hb, add, (zero, zero))
+        own = jnp.sum(own, axis=0, keepdims=True)
+        slope = jnp.sum(slope, axis=0, keepdims=True)
+        line = lax.broadcasted_iota(jnp.int32, (8, W), 0)
+        total = exchange(c, jnp.where(line == 0, own, slope))
+        scale = jnp.sqrt(total[0:1, :]) * lax.rsqrt(total[1:2, :] + 1e-06)
+        def step(i, carry):
+            rows = pl.ds(up(i * hb, hb), hb)
+            state, stepped = update(totd[rows, :] * scale, md[rows, :], ed[rows, :])
+            td[rows, :] = state
+            sd[rows, :] = stepped
+            cd[rows, pl.ds(up(me * W, 128), W)] = stepped.astype(bf16)
+            return carry
+        lax.fori_loop(0, H // hb, step, 0)
+
+    def upper(c):
+        base, rb = (c - 1) * rc, 16
+        lane = lax.broadcasted_iota(jnp.int32, (rb, 128), 1)
+        sums = []
+        for i in range(rc // rb):
+            rows = pl.ds(base + i * rb, rb)
+            acc = ru[0, rows, :].astype(f32)
+            for s in range(1, n):
+                acc = acc + ru[s, rows, :].astype(f32)
+            acc = acc * rate
+            totu[rows, :] = acc
+            w = mu[rows, :]
+            sums.append(
+                jnp.where(
+                    lane == 0,
+                    jnp.sum(w * w, axis=1, keepdims=True),
+                    jnp.sum(acc * acc, axis=1, keepdims=True),
+                )
+            )
+        square = jnp.concatenate(sums * (128 // rc), axis=0)
+        total = exchange(c, square.T[0:8, :])
+        back = jnp.concatenate([total] * 16, axis=0).T
+        scales = jnp.sqrt(back[:, 0:1]) * lax.rsqrt(back[:, 1:2] + 1e-06)
+        for i in range(rc // rb):
+            rows = pl.ds(base + i * rb, rb)
+            state, stepped = update(
+                totu[rows, :] * scales[i * rb : (i + 1) * rb, :], mu[rows, :], eu[rows, :]
+            )
+            tu[rows, :] = state
+            su[rows, :] = stepped
+            cu[pl.ds(up(me * R + base + i * rb, 16), rb), :] = stepped.astype(bf16)
+
+    def az_copy(c, o):
+        b = block_of(c, me)
+        return remote(b, b, azs.at[c, o], azr.at[c, z], (lax.rem(z + o, Z) * Y + y, tp))
+
+    def ay_copy(c, q, o):
+        b = block_of(c, q * Y + y)
+        return remote(b, b, ays.at[c, q, o], ayr.at[c, q, y], (z * Y + lax.rem(y + o, Y), tp))
+
+    def gather_start(c):
+        for o in range(1, Z):
+            az_copy(c, o).start()
+        for o in range(1, Y):
+            ay_copy(c, z, o).start()
+
+    def forward(c):
+        for o in range(1, Z):
+            q = lax.rem(z + o, Z)
+            b = block_of(c, q * Y + y)
+            remote(b, b, azs.at[c, 0], azr.at[c, q], (q * Y + y, tp)).wait_recv()
+            for v in range(1, Y):
+                ay_copy(c, q, v).start()
+
+    def norm():
+        for s in peers:
+            remote(pn, rn.at[s], nms.at[0], nmr.at[s], (s, tp)).wait_recv()
+        total = rn[0, 0:n, :]
+        for s in range(1, n):
+            total = total + rn[s, 0:n, :]
+        master = jnp.concatenate([rn[s, n : n + 1, :] for s in range(n)], axis=0)
+        memory = jnp.concatenate([rn[s, n + 1 : n + 2, :] for s in range(n)], axis=0)
+        state, stepped = update(total * rate, master, memory)
+        cn[...] = stepped.astype(bf16)
+        line = lax.broadcasted_iota(jnp.int32, stepped.shape, 0)
+        sn[...] = jnp.sum(jnp.where(line == me, stepped, 0.0), axis=0, keepdims=True)
+        tn[...] = jnp.sum(jnp.where(line == me, state, 0.0), axis=0, keepdims=True)
+
+    barrier = pltpu.get_barrier_semaphore()
+    for d in peers:
+        pl.semaphore_signal(barrier, inc=1, device_id=(d, tp), device_id_type=MESH)
+    for t in tpeers:
+        pl.semaphore_signal(barrier, inc=1, device_id=(me, t), device_id_type=MESH)
+    for c in range(K + 1):
+        local_copy(c).start()
+    rn[me] = pn[...]
+    pl.semaphore_wait(barrier, n + T - 2)
+
+    rs_start(0)
+    for o, d in enumerate(peers):
+        remote(pn, rn.at[me], nms.at[o], nmr.at[me], (d, tp)).start()
+    rs_start(1)
+    norm()
+    rs_wait(0)
+    down()
+    gather_start(0)
+    for c in range(1, K + 1):
+        if c < K:
+            rs_start(c + 1)
+        rs_wait(c)
+        upper(c)
+        gather_start(c)
+        forward(c - 1)
+    forward(K)
+
+    for o, d in enumerate(peers):
+        remote(pn, rn.at[me], nms.at[o], nmr.at[me], (d, tp)).wait_send()
+    for c in range(K + 1):
+        for o, d in enumerate(peers):
+            rs_copy(c, o, d).wait_send()
+        for o, t in enumerate(tpeers):
+            nx_copy(c, o, t).wait_send()
+        for o in range(1, Z):
+            az_copy(c, o).wait_send()
+        for q in range(Z):
+            for o in range(1, Y):
+                ay_copy(c, q, o).wait_send()
+                v = lax.rem(y + o, Y)
+                b = block_of(c, q * Y + v)
+                remote(b, b, ays.at[c, q, 0], ayr.at[c, q, v], (z * Y + v, tp)).wait_recv()
+
+
+def fused(pu, pd, pn, mu, md, mn, eu, ed, en):
+    n, T = lax.axis_size("dp"), lax.axis_size("tp")
+    Y = 2 if n % 2 == 0 else 1
+    Z = n // Y
+    (R, C), (H, W) = mu.shape, md.shape
+    K = 2 if R % 32 == 0 else 1
+    V = mn.shape[0]
+    rows = -(-(n + 2) // 8) * 8
+    packed = jnp.concatenate(
+        [
+            pn[0].astype(f32).reshape(n, V),
+            mn[None],
+            en[None],
+            jnp.zeros((rows - n - 2, V), f32),
+        ]
+    )
+    hbm = pl.BlockSpec(memory_space=pl.ANY)
+    vmem = pl.BlockSpec(memory_space=pltpu.VMEM)
+    shape = jax.ShapeDtypeStruct
+    dma = pltpu.SemaphoreType.DMA
+    outs = pl.pallas_call(
+        functools.partial(kernel, n, T, Y, K),
+        out_shape=(
+            shape((H, n * W), bf16),
+            shape((n * R, C), bf16),
+            shape((n, V), bf16),
+            shape((H, W), f32),
+            shape((R, C), f32),
+            shape((1, V), f32),
+            shape((H, W), f32),
+            shape((R, C), f32),
+            shape((1, V), f32),
+        ),
+        in_specs=[hbm, hbm] + [vmem] * 5,
+        out_specs=[vmem] * 9,
+        scratch_shapes=[
+            pltpu.VMEM((n, H, W), bf16),
+            pltpu.VMEM((n, R, C), bf16),
+            pltpu.VMEM((n, rows, V), f32),
+            pltpu.VMEM((H, W), f32),
+            pltpu.VMEM((R, C), f32),
+            pltpu.VMEM((K + 1, 8, 128), f32),
+            pltpu.VMEM((K + 1, T, 8, 128), f32),
+            dma((K + 1,)),
+            dma((n,)),
+            dma((n,)),
+            dma((K + 1, n)),
+            dma((K + 1, n)),
+            dma((K + 1, T)),
+            dma((K + 1, T)),
+            dma((K + 1, Z)),
+            dma((K + 1, Z)),
+            dma((K + 1, Z, Y)),
+            dma((K + 1, Z, Y)),
+        ],
+        compiler_params=pltpu.CompilerParams(
+            collective_id=0, has_side_effects=True, vmem_limit_bytes=56 * 1024 * 1024
+        ),
+    )(pd, pu, packed, md, ed, mu, eu)
+    cd, cu, cn, sd, su, sn, td, tu, tn = outs
+    return cu, cd, cn.reshape(-1), su, sd, sn.reshape(-1), tu, td, tn.reshape(-1)
 
 
 def local(
@@ -66,9 +355,16 @@
     )
 
 
+def either(*args):
+    (R, C), (H, W) = args[3].shape, args[4].shape
+    V = args[5].shape[0]
+    aligned = R == 128 and W == 128 and V == 128 and C % 128 == 0 and H % 128 == 0
+    return fused(*args) if aligned else local(*args)
+
+
 def solution(mesh):
     return jax.shard_map(
-        local,
+        either,
         mesh=mesh,
         in_specs=(
             P("dp", None, "tp"),

time: 316 us -> 175 us (0.55)
  the two profiles are of different devices: /device:TPU:0 before, /device:TPU:24 now
where the time goes in v1:
time: 175 us; the launch traced here: 174 us
  Pallas kernels  162 us (93%)
  local copies, waits for them, and re-layouts  9.43 us (5%)
  other arithmetic  2.03 us (1%)
    pallas_call x1, Pallas kernels, fused(): pl.pallas_call(functools.partial(kernel, n, T, Y, K), out_shape=(shape((H...  162 us
    unnamed x25, local copies, waits for them, and re-layouts  9.36 us

profile of v1, /device:TPU:24, one launch (start us, length us, event | category | flops | bytes accessed | tf_op | source)
XLA Modules:
  0.0 174.4 jit_solution(7028095691046532284)
XLA Ops:
  0.7 0.1 pad.3.clone
  0.7 0.7 convert_element_type.9
  1.4 1.3 maximum_maximum_fusion.pn
  2.8 162.2 %shard_map.160 = (bf16[1024,1024]{1,0:T(8,128)(2,1)}, bf16[1024,1024]{1,0:T(8,128)(2,1)}, bf16[8,128]{1,0:T(8,128)(2,1)}, f32[1024,128]{1,0:T(8,128)}, f32[128,1...) custom-call(bf16[1,1024,1024]{2,1,0:T(8,128)(2,1)} %pd.1, ...), custom_call_target="tpu_custom_call" | custom-call | tf_op jit(solution)/shard_map/pallas_call | solution.py:256
  165.0 0.0 copy-start
  165.0 3.2 %copy.27 = bf16[1024,1024]{1,0:T(8,128)(2,1)} copy(bf16[1024,1024]{1,0:T(8,128)(2,1)} %get-tuple-element.36) | data formatting | bytes 4194304
  168.2 0.0 copy-done
  168.3 0.0 copy-start.5
  168.3 0.0 copy-start.4
  168.3 0.0 copy-start.3
  168.3 1.3 copy.28
  169.6 0.0 copy-done.5
  169.6 0.0 copy-start.7
  169.6 0.0 copy-start.2
  169.6 0.0 copy-start.1
  169.6 0.6 copy.29
  170.2 0.0 copy-done.4
  170.2 0.0 copy-start.6
  170.2 0.8 copy.30
  171.0 0.0 copy-done.3
  171.0 0.8 copy.31
  171.8 0.0 copy-done.7
  171.8 0.5 copy.32
  172.3 0.0 copy-done.2
  172.3 0.8 copy.33
  173.1 0.0 copy-done.1
  173.1 0.8 copy.34
  173.9 0.0 copy-done.6
  173.9 0.5 copy.35
  (1 shorter events, 0.0 us)
Async XLA Ops:
  165.0 3.2 %copy-start = (bf16[1024,1024]{1,0:T(8,128)(2,1)S(1)}, bf16[1024,1024]{1,0:T(8,128)(2,1)}, u32[]{:S(2)}) copy-start(bf16[1024,1024]{1,0:T(8,128)(2,1)} %get-tuple-element.37) | copy-start | bytes 6291460
  168.3 1.3 copy-start.5
  168.3 1.9 %copy-start.4 = (f32[128,1024]{1,0:T(8,128)S(1)}, f32[128,1024]{1,0:T(8,128)}, u32[]{:S(2)}) copy-start(f32[128,1024]{1,0:T(8,128)} %get-tuple-element.39) | copy-start | bytes 1572868
  168.3 2.7 %copy-start.3 = (f32[1024,128]{1,0:T(8,128)S(1)}, f32[1024,128]{1,0:T(8,128)}, u32[]{:S(2)}) copy-start(f32[1024,128]{1,0:T(8,128)} %get-tuple-element.40) | copy-start | bytes 1572868
  169.6 2.2 %copy-start.7 = (f32[1,128]{1,0:T(1,128)S(1)}, f32[1,128]{1,0:T(1,128)}, u32[]{:S(2)}) copy-start(f32[1,128]{1,0:T(1,128)} %get-tuple-element.23) | copy-start | bytes 1540
  169.6 2.7 %copy-start.2 = (f32[128,1024]{1,0:T(8,128)S(1)}, f32[128,1024]{1,0:T(8,128)}, u32[]{:S(2)}) copy-start(f32[128,1024]{1,0:T(8,128)} %get-tuple-element.42) | copy-start | bytes 1572868
  169.6 3.5 %copy-start.1 = (f32[1024,128]{1,0:T(8,128)S(1)}, f32[1024,128]{1,0:T(8,128)}, u32[]{:S(2)}) copy-start(f32[1024,128]{1,0:T(8,128)} %get-tuple-element.43) | copy-start | bytes 1572868
  170.2 3.7 %copy-start.6 = (f32[1,128]{1,0:T(1,128)S(1)}, f32[1,128]{1,0:T(1,128)}, u32[]{:S(2)}) copy-start(f32[1,128]{1,0:T(1,128)} %get-tuple-element.26) | copy-start | bytes 1540

commit v2 on v1

--- a/solution.py
+++ b/solution.py
@@ -18,18 +18,20 @@
     n, T, Y, K,
     pd, pu, pn, md, ed, mu, eu,
     cd, cu, cn, sd, su, sn, td, tu, tn,
-    rd, ru, rn, totd, totu, nsend, nrecv,
-    loc, nms, nmr, rss, rsr, nxs, nxr, azs, azr, ays, ayr,
+    od, yd, sumd, leftd, rightd, ou, yu, sumu, leftu, rightu,
+    rn, totd, totu, nsend, nrecv,
+    loc, nms, nmr, yss, ysr, zss, zlr, zrr, nxs, nxr, als, ars, azr, ays, ayr,
 ):
     Z = n // Y
     me = lax.axis_index("dp")
     tp = lax.axis_index("tp")
     z, y = me // Y, me % Y
-    W = rd.shape[2]
-    R = ru.shape[1]
-    H = rd.shape[1]
+    H, W = md.shape
+    R = mu.shape[0]
     rc = R // K
     rate = n ** -0.5
+    hb, rb = 128, 16
+    order = list(range(K + 1))
 
     def remote(src, dst, s, r, dev):
         return pltpu.make_async_remote_copy(
@@ -41,36 +43,129 @@
 
     peers = [lax.rem(me + o, n) for o in range(1, n)]
     tpeers = [lax.rem(tp + o, T) for o in range(1, T)]
+    right, left = (lax.rem(z + 1, Z) * Y + y, tp), (lax.rem(z + Z - 1, Z) * Y + y, tp)
+    other = (z * Y + lax.rem(y + 1, Y), tp)
 
     def src_of(c, d):
         if c == 0:
             return pd.at[0, :, pl.ds(up(d * W, 128), W)]
         return pu.at[0, pl.ds(up(d * R + (c - 1) * rc, 16), rc), :]
 
-    def slot_of(c, s):
+    def slot(c, down_ref, up_ref, q):
         if c == 0:
-            return rd.at[s]
-        return ru.at[s, pl.ds((c - 1) * rc, rc), :]
+            return down_ref.at[q]
+        return up_ref.at[q, pl.ds((c - 1) * rc, rc), :]
 
     def block_of(c, d):
         if c == 0:
             return cd.at[:, pl.ds(up(d * W, 128), W)]
         return cu.at[pl.ds(up(d * R + (c - 1) * rc, 16), rc), :]
 
-    def local_copy(c):
-        return pltpu.make_async_copy(src_of(c, me), slot_of(c, me), loc.at[c])
-
-    def rs_copy(c, o, d):
-        return remote(src_of(c, d), slot_of(c, me), rss.at[c, o], rsr.at[c, me], (d, tp))
-
-    def rs_start(c):
-        for o, d in enumerate(peers):
-            rs_copy(c, o, d).start()
-
-    def rs_wait(c):
-        local_copy(c).wait()
-        for s in peers:
-            remote(slot_of(c, s), slot_of(c, s), rss.at[c, 0], rsr.at[c, s], (s, tp)).wait_recv()
+    def rows_of(c, i):
+        if c == 0:
+            return pl.ds(up(i * hb, hb), hb)
+        return pl.ds(up((c - 1) * rc + i * rb, rb), rb)
+
+    def count(c):
+        return H // hb if c == 0 else rc // rb
+
+    def local_copy(c, q):
+        return pltpu.make_async_copy(src_of(c, q * Y + y), slot(c, od, ou, q), loc.at[c, q])
+
+    def y_copy(c, q):
+        d = q * Y + lax.rem(y + 1, Y)
+        return remote(src_of(c, d), slot(c, yd, yu, q), yss.at[c, q], ysr.at[c, q], other)
+
+    def y_wait(c, q):
+        local_copy(c, q).wait()
+        if Y > 1:
+            y_copy(c, q).wait_recv()
+
+    def y_start(c, qs):
+        for q in qs:
+            local_copy(c, q).start()
+            if Y > 1:
+                y_copy(c, q).start()
+
+    def pair(c, q, rows):
+        o, v = (od, yd) if c == 0 else (ou, yu)
+        total = o[q, rows, :].astype(f32)
+        if Y > 1:
+            total = total + v[q, rows, :].astype(f32)
+        return total
+
+    def to_right(c, q):
+        return remote(slot(c, sumd, sumu, q), slot(c, leftd, leftu, q), zss.at[c, q], zlr.at[c, q], right)
+
+    def to_left(c, q):
+        return remote(slot(c, sumd, sumu, q), slot(c, rightd, rightu, q), zss.at[c, q], zrr.at[c, q], left)
+
+    def relay(c, q, rightward, first):
+        out = sumd if c == 0 else sumu
+        y_wait(c, q)
+        if rightward:
+            held = leftd if c == 0 else leftu
+            if not first:
+                to_right(c, q).wait_recv()
+        else:
+            held = rightd if c == 0 else rightu
+            if not first:
+                to_left(c, q).wait_recv()
+
+        def add(i, carry):
+            rows = rows_of(c, i)
+            total = pair(c, q, rows)
+            if not first:
+                total = total + held[q, rows, :]
+            out[q, rows, :] = total
+            return carry
+
+        lax.fori_loop(0, count(c), add, 0)
+        (to_right if rightward else to_left)(c, q).start()
+
+    def ends(c):
+        if Z == 1:
+            return
+
+        @pl.when(z == 0)
+        def _():
+            for q in range(Z - 1, 0, -1):
+                relay(c, q, True, True)
+
+        @pl.when(z == Z - 1)
+        def _():
+            for q in range(Z - 1):
+                relay(c, q, False, True)
+
+    def middle(c):
+        for k in range(Z - 1):
+            q = Z - 1 - k
+
+            @pl.when((z > 0) & (z < q))
+            def _():
+                relay(c, q, True, False)
+
+            @pl.when((z < Z - 1) & (z > k))
+            def _():
+                relay(c, k, False, False)
+
+    def final_wait(c):
+        y_wait(c, z)
+
+        @pl.when(z > 0)
+        def _():
+            to_right(c, z).wait_recv()
+
+        @pl.when(z < Z - 1)
+        def _():
+            to_left(c, z).wait_recv()
+
+    def whole(c, rows):
+        l, r = (leftd, rightd) if c == 0 else (leftu, rightu)
+        total = pair(c, z, rows)
+        total = total + jnp.where(z > 0, l[z, rows, :], 0.0)
+        total = total + jnp.where(z < Z - 1, r[z, rows, :], 0.0)
+        return total * rate
 
     def nx_copy(c, o, t):
         return remote(nsend.at[c], nrecv.at[c, tp], nxs.at[c, o], nxr.at[c, tp], (me, t))
@@ -92,19 +187,18 @@
         return state, master - learn_rate * m * lax.rsqrt(state + 1e-06)
 
     def down():
-        c, hb = 0, 128
+        c = 0
+
         def add(i, carry):
-            rows = pl.ds(up(i * hb, hb), hb)
-            acc = rd[0, rows, :].astype(f32)
-            for s in range(1, n):
-                acc = acc + rd[s, rows, :].astype(f32)
-            acc = acc * rate
+            rows = rows_of(c, i)
+            acc = whole(c, rows)
             totd[rows, :] = acc
             w = md[rows, :]
             return (
                 carry[0] + jnp.sum((w * w).reshape(hb // 8, 8, W), axis=0),
                 carry[1] + jnp.sum((acc * acc).reshape(hb // 8, 8, W), axis=0),
             )
+
         zero = jnp.zeros((8, W), f32)
         own, slope = lax.fori_loop(0, H // hb, add, (zero, zero))
         own = jnp.sum(own, axis=0, keepdims=True)
@@ -112,25 +206,23 @@
         line = lax.broadcasted_iota(jnp.int32, (8, W), 0)
         total = exchange(c, jnp.where(line == 0, own, slope))
         scale = jnp.sqrt(total[0:1, :]) * lax.rsqrt(total[1:2, :] + 1e-06)
+
         def step(i, carry):
-            rows = pl.ds(up(i * hb, hb), hb)
+            rows = rows_of(c, i)
             state, stepped = update(totd[rows, :] * scale, md[rows, :], ed[rows, :])
             td[rows, :] = state
             sd[rows, :] = stepped
             cd[rows, pl.ds(up(me * W, 128), W)] = stepped.astype(bf16)
             return carry
+
         lax.fori_loop(0, H // hb, step, 0)
 
     def upper(c):
-        base, rb = (c - 1) * rc, 16
         lane = lax.broadcasted_iota(jnp.int32, (rb, 128), 1)
         sums = []
         for i in range(rc // rb):
-            rows = pl.ds(base + i * rb, rb)
-            acc = ru[0, rows, :].astype(f32)
-            for s in range(1, n):
-                acc = acc + ru[s, rows, :].astype(f32)
-            acc = acc * rate
+            rows = rows_of(c, i)
+            acc = whole(c, rows)
             totu[rows, :] = acc
             w = mu[rows, :]
             sums.append(
@@ -145,35 +237,66 @@
         back = jnp.concatenate([total] * 16, axis=0).T
         scales = jnp.sqrt(back[:, 0:1]) * lax.rsqrt(back[:, 1:2] + 1e-06)
         for i in range(rc // rb):
-            rows = pl.ds(base + i * rb, rb)
+            rows = rows_of(c, i)
             state, stepped = update(
                 totu[rows, :] * scales[i * rb : (i + 1) * rb, :], mu[rows, :], eu[rows, :]
             )
             tu[rows, :] = state
             su[rows, :] = stepped
-            cu[pl.ds(up(me * R + base + i * rb, 16), rb), :] = stepped.astype(bf16)
-
-    def az_copy(c, o):
-        b = block_of(c, me)
-        return remote(b, b, azs.at[c, o], azr.at[c, z], (lax.rem(z + o, Z) * Y + y, tp))
-
-    def ay_copy(c, q, o):
+            cu[pl.ds(up(me * R + (c - 1) * rc + i * rb, 16), rb), :] = stepped.astype(bf16)
+
+    def final(c):
+        final_wait(c)
+        if c == 0:
+            down()
+        else:
+            upper(c)
+
+    def move(c, q, s, dev):
         b = block_of(c, q * Y + y)
-        return remote(b, b, ays.at[c, q, o], ayr.at[c, q, y], (z * Y + lax.rem(y + o, Y), tp))
+        return remote(b, b, s.at[c, q], azr.at[c, q], dev)
+
+    def y_move(c, q, v):
+        b = block_of(c, q * Y + v)
+        return remote(b, b, ays.at[c, q], ayr.at[c, q], other)
 
     def gather_start(c):
-        for o in range(1, Z):
-            az_copy(c, o).start()
-        for o in range(1, Y):
-            ay_copy(c, z, o).start()
+        @pl.when(z < Z - 1)
+        def _():
+            move(c, z, ars, right).start()
+
+        @pl.when(z > 0)
+        def _():
+            move(c, z, als, left).start()
+
+        if Y > 1:
+            y_move(c, z, y).start()
 
     def forward(c):
-        for o in range(1, Z):
-            q = lax.rem(z + o, Z)
-            b = block_of(c, q * Y + y)
-            remote(b, b, azs.at[c, 0], azr.at[c, q], (q * Y + y, tp)).wait_recv()
-            for v in range(1, Y):
-                ay_copy(c, q, v).start()
+        for k in range(1, Z):
+            @pl.when(z >= k)
+            def _():
+                q = z - k
+                move(c, q, ars, right).wait_recv()
+
+                @pl.when(z < Z - 1)
+                def _():
+                    move(c, q, ars, right).start()
+
+                if Y > 1:
+                    y_move(c, q, y).start()
+
+            @pl.when(z + k < Z)
+            def _():
+                q = z + k
+                move(c, q, als, left).wait_recv()
+
+                @pl.when(z > 0)
+                def _():
+                    move(c, q, als, left).start()
+
+                if Y > 1:
+                    y_move(c, q, y).start()
 
     def norm():
         for s in peers:
@@ -194,43 +317,64 @@
         pl.semaphore_signal(barrier, inc=1, device_id=(d, tp), device_id_type=MESH)
     for t in tpeers:
         pl.semaphore_signal(barrier, inc=1, device_id=(me, t), device_id_type=MESH)
-    for c in range(K + 1):
-        local_copy(c).start()
     rn[me] = pn[...]
     pl.semaphore_wait(barrier, n + T - 2)
 
-    rs_start(0)
+    far = []
+    for k in range((Z + 1) // 2):
+        far += [Z - 1 - k] + ([k] if k != Z - 1 - k else [])
+
+    @pl.when(2 * z < Z)
+    def _():
+        for c in order:
+            y_start(c, far)
+
+    @pl.when(2 * z >= Z)
+    def _():
+        for c in order:
+            y_start(c, [Z - 1 - q for q in far])
+
     for o, d in enumerate(peers):
         remote(pn, rn.at[me], nms.at[o], nmr.at[me], (d, tp)).start()
-    rs_start(1)
-    norm()
-    rs_wait(0)
-    down()
-    gather_start(0)
-    for c in range(1, K + 1):
-        if c < K:
-            rs_start(c + 1)
-        rs_wait(c)
-        upper(c)
+
+    ends(order[0])
+    middle(order[0])
+    for i, c in enumerate(order):
+        last = i + 1 == len(order)
+        if not last:
+            ends(order[i + 1])
+        if i >= 1:
+            forward(order[i - 1])
+        final(c)
         gather_start(c)
-        forward(c - 1)
-    forward(K)
+        if i == 0:
+            norm()
+        if not last:
+            middle(order[i + 1])
+    forward(order[-1])
 
     for o, d in enumerate(peers):
         remote(pn, rn.at[me], nms.at[o], nmr.at[me], (d, tp)).wait_send()
-    for c in range(K + 1):
-        for o, d in enumerate(peers):
-            rs_copy(c, o, d).wait_send()
+    for c in order:
         for o, t in enumerate(tpeers):
             nx_copy(c, o, t).wait_send()
-        for o in range(1, Z):
-            az_copy(c, o).wait_send()
         for q in range(Z):
-            for o in range(1, Y):
-                ay_copy(c, q, o).wait_send()
-                v = lax.rem(y + o, Y)
-                b = block_of(c, q * Y + v)
-                remote(b, b, ays.at[c, q, 0], ayr.at[c, q, v], (z * Y + v, tp)).wait_recv()
+            if Y > 1:
+                y_copy(c, q).wait_send()
+                y_move(c, q, y).wait_send()
+                y_move(c, q, lax.rem(y + 1, Y)).wait_recv()
+
+            @pl.when(z != q)
+            def _():
+                to_right(c, q).wait_send()
+
+            @pl.when((z >= q) & (z < Z - 1))
+            def _():
+                move(c, q, ars, right).wait_send()
+
+            @pl.when((z <= q) & (z > 0))
+            def _():
+                move(c, q, als, left).wait_send()
 
 
 def fused(pu, pd, pn, mu, md, mn, eu, ed, en):
@@ -269,24 +413,36 @@
         in_specs=[hbm, hbm] + [vmem] * 5,
         out_specs=[vmem] * 9,
         scratch_shapes=[
-            pltpu.VMEM((n, H, W), bf16),
-            pltpu.VMEM((n, R, C), bf16),
+            pltpu.VMEM((Z, H, W), bf16),
+            pltpu.VMEM((Z, H, W), bf16),
+            pltpu.VMEM((Z, H, W), f32),
+            pltpu.VMEM((Z, H, W), f32),
+            pltpu.VMEM((Z, H, W), f32),
+            pltpu.VMEM((Z, R, C), bf16),
+            pltpu.VMEM((Z, R, C), bf16),
+            pltpu.VMEM((Z, R, C), f32),
+            pltpu.VMEM((Z, R, C), f32),
+            pltpu.VMEM((Z, R, C), f32),
             pltpu.VMEM((n, rows, V), f32),
             pltpu.VMEM((H, W), f32),
             pltpu.VMEM((R, C), f32),
             pltpu.VMEM((K + 1, 8, 128), f32),
             pltpu.VMEM((K + 1, T, 8, 128), f32),
-            dma((K + 1,)),
+            dma((K + 1, Z)),
             dma((n,)),
             dma((n,)),
-            dma((K + 1, n)),
-            dma((K + 1, n)),
+            dma((K + 1, Z)),
+            dma((K + 1, Z)),
+            dma((K + 1, Z)),
+            dma((K + 1, Z)),
+            dma((K + 1, Z)),
             dma((K + 1, T)),
             dma((K + 1, T)),
             dma((K + 1, Z)),
             dma((K + 1, Z)),
-            dma((K + 1, Z, Y)),
-            dma((K + 1, Z, Y)),
+            dma((K + 1, Z)),
+            dma((K + 1, Z)),
+            dma((K + 1, Z)),
         ],
         compiler_params=pltpu.CompilerParams(
             collective_id=0, has_side_effects=True, vmem_limit_bytes=56 * 1024 * 1024

time: 175 us -> 166 us (0.949)
  the two profiles are of different devices: /device:TPU:24 before, /device:TPU:0 now
where the time goes in v2:
time: 166 us
  Pallas kernels  154 us (93%)
  local copies, waits for them, and re-layouts  9.43 us (6%)
  other arithmetic  2.03 us (1%)
    pallas_call x1, Pallas kernels, fused(): pl.pallas_call(functools.partial(kernel, n, T, Y, K), out_shape=(shape((H...  154 us
    unnamed x25, local copies, waits for them, and re-layouts  9.36 us

profile of v2, /device:TPU:0, one launch (start us, length us, event | category | flops | bytes accessed | tf_op | source)
XLA Modules:
  0.0 166.0 jit_solution(42719743559757851)
XLA Ops:
  0.7 0.1 pad.3.clone
  0.7 0.7 convert_element_type.9
  1.4 1.3 maximum_maximum_fusion.pn
  2.8 153.8 %shard_map.160 = (bf16[1024,1024]{1,0:T(8,128)(2,1)}, bf16[1024,1024]{1,0:T(8,128)(2,1)}, bf16[8,128]{1,0:T(8,128)(2,1)}, f32[1024,128]{1,0:T(8,128)}, f32[128,1...) custom-call(bf16[1,1024,1024]{2,1,0:T(8,128)(2,1)} %pd.1, ...), custom_call_target="tpu_custom_call" | custom-call | tf_op jit(solution)/shard_map/pallas_call | solution.py:400
  156.6 0.0 copy-start
  156.6 3.2 %copy.27 = bf16[1024,1024]{1,0:T(8,128)(2,1)} copy(bf16[1024,1024]{1,0:T(8,128)(2,1)} %get-tuple-element.36) | data formatting | bytes 4194304
  159.9 0.0 copy-done
  159.9 0.0 copy-start.5
  159.9 0.0 copy-start.4
  159.9 0.0 copy-start.3
  159.9 1.3 copy.28
  161.2 0.0 copy-done.5
  161.2 0.0 copy-start.7
  161.2 0.0 copy-start.2
  161.2 0.0 copy-start.1
  161.2 0.6 copy.29
  161.8 0.0 copy-done.4
  161.8 0.0 copy-start.6
  161.8 0.8 copy.30
  162.6 0.0 copy-done.3
  162.6 0.8 copy.31
  163.4 0.0 copy-done.7
  163.4 0.5 copy.32
  163.9 0.0 copy-done.2
  163.9 0.8 copy.33
  164.7 0.0 copy-done.1
  164.7 0.8 copy.34
  165.5 0.0 copy-done.6
  165.5 0.5 copy.35
  (1 shorter events, 0.0 us)
Async XLA Ops:
  156.6 3.2 %copy-start = (bf16[1024,1024]{1,0:T(8,128)(2,1)S(1)}, bf16[1024,1024]{1,0:T(8,128)(2,1)}, u32[]{:S(2)}) copy-start(bf16[1024,1024]{1,0:T(8,128)(2,1)} %get-tuple-element.37) | copy-start | bytes 6291460
  159.9 1.3 copy-start.5
  159.9 1.9 %copy-start.4 = (f32[128,1024]{1,0:T(8,128)S(1)}, f32[128,1024]{1,0:T(8,128)}, u32[]{:S(2)}) copy-start(f32[128,1024]{1,0:T(8,128)} %get-tuple-element.39) | copy-start | bytes 1572868
  159.9 2.7 %copy-start.3 = (f32[1024,128]{1,0:T(8,128)S(1)}, f32[1024,128]{1,0:T(8,128)}, u32[]{:S(2)}) copy-start(f32[1024,128]{1,0:T(8,128)} %get-tuple-element.40) | copy-start | bytes 1572868
  161.2 2.2 %copy-start.7 = (f32[1,128]{1,0:T(1,128)S(1)}, f32[1,128]{1,0:T(1,128)}, u32[]{:S(2)}) copy-start(f32[1,128]{1,0:T(1,128)} %get-tuple-element.23) | copy-start | bytes 1540
  161.2 2.7 %copy-start.2 = (f32[128,1024]{1,0:T(8,128)S(1)}, f32[128,1024]{1,0:T(8,128)}, u32[]{:S(2)}) copy-start(f32[128,1024]{1,0:T(8,128)} %get-tuple-element.42) | copy-start | bytes 1572868
  161.2 3.5 %copy-start.1 = (f32[1024,128]{1,0:T(8,128)S(1)}, f32[1024,128]{1,0:T(8,128)}, u32[]{:S(2)}) copy-start(f32[1024,128]{1,0:T(8,128)} %get-tuple-element.43) | copy-start | bytes 1572868
  161.8 3.7 %copy-start.6 = (f32[1,128]{1,0:T(1,128)S(1)}, f32[1,128]{1,0:T(1,128)}, u32[]{:S(2)}) copy-start(f32[1,128]{1,0:T(1,128)} %get-tuple-element.26) | copy-start | bytes 1540

commit v3 on v2

--- a/solution.py
+++ b/solution.py
@@ -14,8 +14,14 @@
 MESH = pl.DeviceIdType.MESH
 
 
+def schedule(D, K):
+    downs, ups = list(range(D)), list(range(D, D + K))
+    plan = [('end', 1), ('end', 0), ('mid', 1), ('sum', (1,)), ('end', 2), ('mid', 0), ('fwd', 1), ('sum', (0,)), ('mid', 2), ('fwd', 0), ('sum', (2,)), ('fwd', 2)]
+    return plan
+
+
 def kernel(
-    n, T, Y, K,
+    n, T, Y, D, K,
     pd, pu, pn, md, ed, mu, eu,
     cd, cu, cn, sd, su, sn, td, tu, tn,
     od, yd, sumd, leftd, rightd, ou, yu, sumu, leftu, rightu,
@@ -31,7 +37,9 @@
     rc = R // K
     rate = n ** -0.5
     hb, rb = 128, 16
-    order = list(range(K + 1))
+    hc = H // D
+    plan = schedule(D, K)
+    order = [p for op, p in plan if op == "end"]
 
     def remote(src, dst, s, r, dev):
         return pltpu.make_async_remote_copy(
@@ -47,27 +55,27 @@
     other = (z * Y + lax.rem(y + 1, Y), tp)
 
     def src_of(c, d):
-        if c == 0:
-            return pd.at[0, :, pl.ds(up(d * W, 128), W)]
-        return pu.at[0, pl.ds(up(d * R + (c - 1) * rc, 16), rc), :]
+        if c < D:
+            return pd.at[0, pl.ds(c * hc, hc), pl.ds(up(d * W, 128), W)]
+        return pu.at[0, pl.ds(up(d * R + (c - D) * rc, 16), rc), :]
 
     def slot(c, down_ref, up_ref, q):
-        if c == 0:
-            return down_ref.at[q]
-        return up_ref.at[q, pl.ds((c - 1) * rc, rc), :]
+        if c < D:
+            return down_ref.at[q, pl.ds(c * hc, hc), :]
+        return up_ref.at[q, pl.ds((c - D) * rc, rc), :]
 
     def block_of(c, d):
-        if c == 0:
-            return cd.at[:, pl.ds(up(d * W, 128), W)]
-        return cu.at[pl.ds(up(d * R + (c - 1) * rc, 16), rc), :]
+        if c < D:
+            return cd.at[pl.ds(c * hc, hc), pl.ds(up(d * W, 128), W)]
+        return cu.at[pl.ds(up(d * R + (c - D) * rc, 16), rc), :]
 
     def rows_of(c, i):
-        if c == 0:
-            return pl.ds(up(i * hb, hb), hb)
-        return pl.ds(up((c - 1) * rc + i * rb, rb), rb)
+        if c < D:
+            return pl.ds(up(c * hc + i * hb, hb), hb)
+        return pl.ds(up((c - D) * rc + i * rb, rb), rb)
 
     def count(c):
-        return H // hb if c == 0 else rc // rb
+        return hc // hb if c < D else rc // rb
 
     def local_copy(c, q):
         return pltpu.make_async_copy(src_of(c, q * Y + y), slot(c, od, ou, q), loc.at[c, q])
@@ -88,7 +96,7 @@
                 y_copy(c, q).start()
 
     def pair(c, q, rows):
-        o, v = (od, yd) if c == 0 else (ou, yu)
+        o, v = (od, yd) if c < D else (ou, yu)
         total = o[q, rows, :].astype(f32)
         if Y > 1:
             total = total + v[q, rows, :].astype(f32)
@@ -101,14 +109,14 @@
         return remote(slot(c, sumd, sumu, q), slot(c, rightd, rightu, q), zss.at[c, q], zrr.at[c, q], left)
 
     def relay(c, q, rightward, first):
-        out = sumd if c == 0 else sumu
+        out = sumd if c < D else sumu
         y_wait(c, q)
         if rightward:
-            held = leftd if c == 0 else leftu
+            held = leftd if c < D else leftu
             if not first:
                 to_right(c, q).wait_recv()
         else:
-            held = rightd if c == 0 else rightu
+            held = rightd if c < D else rightu
             if not first:
                 to_left(c, q).wait_recv()
 
@@ -161,7 +169,7 @@
             to_left(c, z).wait_recv()
 
     def whole(c, rows):
-        l, r = (leftd, rightd) if c == 0 else (leftu, rightu)
+        l, r = (leftd, rightd) if c < D else (leftu, rightu)
         total = pair(c, z, rows)
         total = total + jnp.where(z > 0, l[z, rows, :], 0.0)
         total = total + jnp.where(z < Z - 1, r[z, rows, :], 0.0)
@@ -190,7 +198,7 @@
         c = 0
 
         def add(i, carry):
-            rows = rows_of(c, i)
+            rows = pl.ds(up(i * hb, hb), hb)
             acc = whole(c, rows)
             totd[rows, :] = acc
             w = md[rows, :]
@@ -208,7 +216,7 @@
         scale = jnp.sqrt(total[0:1, :]) * lax.rsqrt(total[1:2, :] + 1e-06)
 
         def step(i, carry):
-            rows = rows_of(c, i)
+            rows = pl.ds(up(i * hb, hb), hb)
             state, stepped = update(totd[rows, :] * scale, md[rows, :], ed[rows, :])
             td[rows, :] = state
             sd[rows, :] = stepped
@@ -233,7 +241,7 @@
                 )
             )
         square = jnp.concatenate(sums * (128 // rc), axis=0)
-        total = exchange(c, square.T[0:8, :])
+        total = exchange(c - D + 1, square.T[0:8, :])
         back = jnp.concatenate([total] * 16, axis=0).T
         scales = jnp.sqrt(back[:, 0:1]) * lax.rsqrt(back[:, 1:2] + 1e-06)
         for i in range(rc // rb):
@@ -243,14 +251,17 @@
             )
             tu[rows, :] = state
             su[rows, :] = stepped
-            cu[pl.ds(up(me * R + (c - 1) * rc + i * rb, 16), rb), :] = stepped.astype(bf16)
-
-    def final(c):
-        final_wait(c)
-        if c == 0:
+            cu[pl.ds(up(me * R + (c - D) * rc + i * rb, 16), rb), :] = stepped.astype(bf16)
+
+    def final(unit):
+        for c in unit:
+            final_wait(c)
+        if unit[0] < D:
             down()
         else:
-            upper(c)
+            upper(unit[0])
+        for c in unit:
+            gather_start(c)
 
     def move(c, q, s, dev):
         b = block_of(c, q * Y + y)
@@ -320,6 +331,9 @@
     rn[me] = pn[...]
     pl.semaphore_wait(barrier, n + T - 2)
 
+    for o, d in enumerate(peers):
+        remote(pn, rn.at[me], nms.at[o], nmr.at[me], (d, tp)).start()
+
     far = []
     for k in range((Z + 1) // 2):
         far += [Z - 1 - k] + ([k] if k != Z - 1 - k else [])
@@ -334,30 +348,18 @@
         for c in order:
             y_start(c, [Z - 1 - q for q in far])
 
-    for o, d in enumerate(peers):
-        remote(pn, rn.at[me], nms.at[o], nmr.at[me], (d, tp)).start()
-
-    ends(order[0])
-    middle(order[0])
-    for i, c in enumerate(order):
-        last = i + 1 == len(order)
-        if not last:
-            ends(order[i + 1])
-        if i >= 1:
-            forward(order[i - 1])
-        final(c)
-        gather_start(c)
-        if i == 0:
+    acts = {"end": ends, "mid": middle, "sum": final, "fwd": forward}
+    for i, (op, p) in enumerate(plan):
+        acts[op](p)
+        if i + 2 == len(plan):
             norm()
-        if not last:
-            middle(order[i + 1])
-    forward(order[-1])
 
     for o, d in enumerate(peers):
         remote(pn, rn.at[me], nms.at[o], nmr.at[me], (d, tp)).wait_send()
-    for c in order:
+    for c in range(K + 1):
         for o, t in enumerate(tpeers):
             nx_copy(c, o, t).wait_send()
+    for c in order:
         for q in range(Z):
             if Y > 1:
                 y_copy(c, q).wait_send()
@@ -375,6 +377,15 @@
             @pl.when((z <= q) & (z > 0))
             def _():
                 move(c, q, als, left).wait_send()
+
+
+def finish(*refs):
+    sems = refs[18]
+    copies = [pltpu.make_async_copy(refs[i], refs[9 + i], sems.at[i]) for i in range(9)]
+    for c in copies:
+        c.start()
+    for c in copies:
+        c.wait()
 
 
 def fused(pu, pd, pn, mu, md, mn, eu, ed, en):
@@ -383,6 +394,7 @@
     Z = n // Y
     (R, C), (H, W) = mu.shape, md.shape
     K = 2 if R % 32 == 0 else 1
+    D = 1 if H % (1 * 128) == 0 else 1
     V = mn.shape[0]
     rows = -(-(n + 2) // 8) * 8
     packed = jnp.concatenate(
@@ -398,7 +410,7 @@
     shape = jax.ShapeDtypeStruct
     dma = pltpu.SemaphoreType.DMA
     outs = pl.pallas_call(
-        functools.partial(kernel, n, T, Y, K),
+        functools.partial(kernel, n, T, Y, D, K),
         out_shape=(
             shape((H, n * W), bf16),
             shape((n * R, C), bf16),
@@ -428,26 +440,33 @@
             pltpu.VMEM((R, C), f32),
             pltpu.VMEM((K + 1, 8, 128), f32),
             pltpu.VMEM((K + 1, T, 8, 128), f32),
-            dma((K + 1, Z)),
+            dma((D + K, Z)),
             dma((n,)),
             dma((n,)),
-            dma((K + 1, Z)),
-            dma((K + 1, Z)),
-            dma((K + 1, Z)),
-            dma((K + 1, Z)),
-            dma((K + 1, Z)),
+            dma((D + K, Z)),
+            dma((D + K, Z)),
+            dma((D + K, Z)),
+            dma((D + K, Z)),
+            dma((D + K, Z)),
             dma((K + 1, T)),
             dma((K + 1, T)),
-            dma((K + 1, Z)),
-            dma((K + 1, Z)),
-            dma((K + 1, Z)),
-            dma((K + 1, Z)),
-            dma((K + 1, Z)),
+            dma((D + K, Z)),
+            dma((D + K, Z)),
+            dma((D + K, Z)),
+            dma((D + K, Z)),
+            dma((D + K, Z)),
         ],
         compiler_params=pltpu.CompilerParams(
             collective_id=0, has_side_effects=True, vmem_limit_bytes=56 * 1024 * 1024
         ),
     )(pd, pu, packed, md, ed, mu, eu)
+    outs = pl.pallas_call(
+        finish,
+        out_shape=[shape(o.shape, o.dtype) for o in outs],
+        in_specs=[vmem] * 9,
+        out_specs=[hbm] * 9,
+        scratch_shapes=[dma((9,))],
+    )(*outs)
     cd, cu, cn, sd, su, sn, td, tu, tn = outs
     return cu, cd, cn.reshape(-1), su, sd, sn.reshape(-1), tu, td, tn.reshape(-1)
 

time: 166 us -> 155 us (0.934)
  local copies, waits for them, and re-layouts: 9.43 us -> 0.08 us
  Pallas kernels: 154 us -> 152 us
    unnamed x25 -> x0, local copies, waits for them, and re-layouts: 9.36 us -> none
    pallas_call x1 -> x2, Pallas kernels: 154 us -> 152 us  [the longest x1 146 us: fused(): pl.pallas_call(functools.partial(kernel, n, T, Y, D, K), out_shape=(shape...]
where the time goes in v3:
time: 155 us; the launch traced here: 154 us
  Pallas kernels  152 us (98%)
  other arithmetic  2.03 us (1%)
    pallas_call x1, Pallas kernels, fused(): pl.pallas_call(functools.partial(kernel, n, T, Y, D, K), out_shape=(shape...  146 us
    pallas_call x1, Pallas kernels, fused(): pl.pallas_call(finish, out_shape=[shape(o.shape, o.dtype) for o in outs],...  5.52 us

profile of v3, /device:TPU:0, one launch (start us, length us, event | category | flops | bytes accessed | tf_op | source)
XLA Modules:
  0.0 154.3 jit_solution(9102274631604152166)
XLA Ops:
  0.7 0.1 pad.3.clone
  0.7 0.7 convert_element_type.9
  1.4 1.3 maximum_maximum_fusion.pn
  2.8 146.0 %shard_map.160 = (bf16[1024,1024]{1,0:T(8,128)(2,1)}, bf16[1024,1024]{1,0:T(8,128)(2,1)}, bf16[8,128]{1,0:T(8,128)(2,1)}, f32[1024,128]{1,0:T(8,128)}, f32[128,1...) custom-call(bf16[1,1024,1024]{2,1,0:T(8,128)(2,1)} %pd.1, ...), custom_call_target="tpu_custom_call" | custom-call | tf_op jit(solution)/shard_map/pallas_call | solution.py:412
  148.8 5.5 %shard_map.161 = (bf16[1024,1024]{1,0:T(8,128)(2,1)}, bf16[1024,1024]{1,0:T(8,128)(2,1)}, bf16[8,128]{1,0:T(8,128)(2,1)}, f32[1024,128]{1,0:T(8,128)}, f32[128,1...) custom-call(bf16[1024,1024]{1,0:T(8,128)(2,1)} %get-tuple-element.27.refs_0_, ...), custom_call_target="tpu_custom_call" | custom-call | tf_op jit(solution)/shard_map/pallas_call | solution.py:463
  (1 shorter events, 0.0 us)
